TPU v7x, 32 devices: a whole 2x2x4 slice. The times are simulated.
32 devices in a mesh: section: 4 (over x, core), tensor: 8 (over z, y).
Axes of the slice: x: 2, y: 2, z: 4, core: 2. Of those that a mesh axis runs over, the one named last changes fastest.
Arguments:
- tokens: bfloat16 [2, 64, 4096], replicated, may hold values from -6 to 6
- norm_gain: bfloat16 [4, 4096], replicated, may hold values from 0.25 to 1.75
- w_in: bfloat16 [4, 2, 14336, 4096], P('section', None, 'tensor'), may hold values from -0.09375 to 0.09375
- w_out: bfloat16 [4, 14336, 4096], P('section', 'tensor'), may hold values from -0.046875 to 0.046875
- backup_in: bfloat16 [4, 2, 14336, 4096], P('section', None, 'tensor'), may hold values from -0.09375 to 0.09375
- backup_out: bfloat16 [4, 14336, 4096], P('section', None, 'tensor'), may hold values from -0.046875 to 0.046875
- layer_group: int32 [4], replicated, may hold values from 0 to 3, as said below
- token_counts: int32 [2], replicated, may hold values from 1 to 64, as said below
Outputs:
- handed: bfloat16 [4, 2, 64, 4096], P('section', None, 'tensor')
Inputs may be any that keep to these rules, and one draw needn't show every extreme that they name: layer_group[l] is l or l + 1. The layers that move up form one run of consecutive layers, at least one, that starts at the layer of the one group left without any layer; that group is never the last one. `token_counts`: rows of a micro-batch from its count on are padding. One micro-batch is full, with 64 real tokens; the other has at most 32.
All inputs are finite; a program needn't handle non-finite values.
Results may differ from a plain program's by a relative error of at most 0.025.
Values may be sent and summed in bfloat16 or wider, within the bound.
A program may use at most 192 MiB of HBM per device.

v0:
```python
import jax
import jax.numpy as jnp
from jax import lax
from jax.sharding import PartitionSpec as P

NORM_EPS = 0.25


def passed_along(block, axis, distance):
    devices = range(lax.axis_size(axis))
    route = [(i - distance, i) for i in devices if i - distance in devices]
    return lax.ppermute(block, axis, route)


def finish_sum(hidden, w_down):
    partial_value = jnp.dot(hidden, w_down, preferred_element_type=jnp.float32)
    return lax.psum(partial_value.astype(jnp.bfloat16), "tensor").astype(jnp.float32)


def finish_columns(hidden, w_down):
    full_hidden = lax.all_gather(hidden, "tensor", axis=1, tiled=True)
    row_count = full_hidden.shape[0]
    blocks = lax.axis_size("tensor")
    block_width = full_hidden.shape[1] // blocks
    pieces = jnp.einsum(
        "rbf,bfd->brd",
        full_hidden.reshape(row_count, blocks, block_width),
        w_down.reshape(blocks, block_width, w_down.shape[1]),
        preferred_element_type=jnp.float32,
    )
    rounded = lax.optimization_barrier(pieces.astype(jnp.bfloat16))
    column_sum = jnp.sum(rounded.astype(jnp.float32), axis=0)
    return lax.all_gather(column_sum.astype(jnp.bfloat16), "tensor", axis=1, tiled=True).astype(
        column_sum.dtype
    )


def apply_layer(current, gain_row, w_pair, finish, w_down, factor):
    wide_x = current.astype(jnp.float32)
    mean_square = jnp.mean(wide_x * wide_x, axis=1, keepdims=True)
    normed = (wide_x * lax.rsqrt(mean_square + NORM_EPS) * gain_row.astype(jnp.float32)).astype(
        jnp.bfloat16
    )
    gate_part = lax.dot_general(
        normed, w_pair[0], (((1,), (1,)), ((), ())), preferred_element_type=jnp.float32
    )
    up_part = lax.dot_general(
        normed, w_pair[1], (((1,), (1,)), ((), ())), preferred_element_type=jnp.float32
    )
    hidden = (jax.nn.silu(gate_part) * up_part).astype(jnp.bfloat16)
    summed = finish(hidden, w_down)
    return (wide_x + factor * summed).astype(jnp.bfloat16)


def select_entry(values, position):
    places = jnp.arange(values.shape[0], dtype=jnp.int32)
    return jnp.sum(jnp.where(places == position, values, 0))


def shards(tokens, norm_gain, w_in, w_out, backup_in, backup_out, layer_group, token_counts):
    section_id = lax.axis_index("section")
    sections = lax.axis_size("section")
    tensor_id = lax.axis_index("tensor")
    tensors = lax.axis_size("tensor")
    batches = tokens.shape[0]
    tok_rows = tokens.shape[1]
    row_share = tok_rows // tensors
    levels = jnp.arange(layer_group.shape[0], dtype=jnp.int32)
    own_keep = select_entry(layer_group, section_id) == section_id
    moved_in = (
        jnp.sum(
            jnp.where(levels == section_id - 1, (layer_group == section_id).astype(jnp.int32), 0)
        )
        > 0
    )
    prior = jnp.maximum(section_id - 1, 0)
    own_gain = lax.dynamic_index_in_dim(norm_gain, section_id, 0, keepdims=True)
    moved_gain = lax.dynamic_index_in_dim(norm_gain, prior, 0, keepdims=True)
    own_slot = (own_gain, w_in[0], finish_sum, w_out[0], own_keep)
    moved_slot = (moved_gain, backup_in[0], finish_columns, backup_out[0], moved_in)
    layer_slots = [moved_slot, own_slot]
    positions = jnp.arange(tok_rows, dtype=jnp.int32)
    batch_ids = jnp.arange(batches, dtype=jnp.int32)
    handed = jnp.zeros((batches, row_share, tokens.shape[2]), jnp.bfloat16)
    arrived = jnp.zeros(tokens.shape[1:], jnp.bfloat16)
    steps_total = sections + batches - 1
    for step_index in range(steps_total):
        step_mb = step_index - section_id
        clipped = jnp.clip(step_mb, 0, batches - 1)
        fresh_input = lax.dynamic_index_in_dim(tokens, clipped, 0, keepdims=False)
        current = jnp.where(section_id == 0, fresh_input, arrived)
        row_count = select_entry(token_counts, clipped)
        row_keep = (positions < row_count).astype(jnp.float32)[:, None]
        for gain_row, w_pair, finish, w_down, active in layer_slots:
            factor = row_keep * active.astype(jnp.float32)
            current = apply_layer(current, gain_row, w_pair, finish, w_down, factor)
        row_block = lax.dynamic_slice_in_dim(current, tensor_id * row_share, row_share, 0)
        in_range = (step_mb >= 0) & (step_mb < batches)
        slot_mask = (batch_ids == step_mb) & in_range
        handed = jnp.where(slot_mask[:, None, None], row_block[None], handed)
        if step_index + 1 < steps_total:
            arrived = passed_along(current, "section", 1)
    return handed[None]


def solution(mesh):
    return jax.shard_map(
        shards,
        mesh=mesh,
        in_specs=(
            P(),
            P(),
            P("section", None, "tensor", None),
            P("section", "tensor", None),
            P("section", None, "tensor", None),
            P("section", None, "tensor"),
            P(),
            P(),
        ),
        out_specs=P("section", None, "tensor", None),
        check_vma=False,
    )
```

profile of v0, /device:TPU:0, one launch (start us, length us, event | category | flops | bytes accessed | tf_op | source)
XLA Modules:
  0.0 1051.5 jit_solution(10932967524345073013)
XLA Ops:
  6.5 1.4 fusion.177
  8.8 8.0 fusion.48
  16.8 8.7 fusion.142
  28.4 46.9 %all-gather.6.cloned.1.call-done = bf16[64,14336]{1,0:T(8,128)(2,1)} async-done(((bf16[64,1792]{1,0:T(8,128)(2,1)}), bf16[64,14336]{1,0:T(8,128)(2,1)}) %all-gather.6.cloned.1.call-update) | async-done | bytes 1835024 | tf_op jit(solution)/shard_map/all_gather | solution.py:21
  75.2 8.3 fusion.162
  83.6 31.4 %all_gather.31 = bf16[64,4096]{1,0:T(8,128)(2,1)S(1)} all-gather(bf16[64,512]{1,0:T(8,128)(2,1)S(1)} %reduce_sum.216), channel_id=1, replica_groups=mesh['section'=4,'tensor'=8] {'tensor'}, dimensions={1}, use_global_device_ids=true | all-gather | bytes 589824 | tf_op jit(solution)/shard_map/all_gather | solution.py:33
  115.4 7.8 fusion.28
  123.2 14.3 %fusion.70 = bf16[64,4096]{1,0:T(8,128)(2,1)} fusion(bf16[1,1792,4096]{2,1,0:T(8,128)(2,1)} %param.11, bf16[1,2,1792,4096]{3,2,1,0:T(8,128)(2,1)} %param.10, f32[64,1792]{1,0:T(8,128)S(1)} %fusion.28, bf16[64,4096]{1,0:T(8,128)(2,1)S(1)} %get-tuple-element.29, f32[4096]{0:T(1024)S(1)} %bitcast.191, f32[64]{0:T(128)S(1)} %add_rsqrt_fusion.8), kind=kOutput, calls=%fused_computation.70 | convolution fusion | flops 1881047040 | bytes 30884096 | tf_op jit(solution)/shard_map/dot_general | solution.py:16
  139.0 70.0 %all-reduce.6.cloned.1.call-done = bf16[64,4096]{1,0:T(8,128)(2,1)} async-done(((bf16[64,4096]{1,0:T(8,128)(2,1)}), bf16[64,4096]{1,0:T(8,128)(2,1)}) %all-reduce.6.cloned.1.call-update) | async-done | bytes 524304 | tf_op jit(solution)/shard_map/psum | solution.py:17
  210.2 1.5 collective-permute-start
  211.7 1.3 collective-permute-done
  213.3 7.8 fusion.46
  221.2 8.6 fusion.139
  230.5 53.2 %all-gather.8.cloned.1.call-done = bf16[64,14336]{1,0:T(8,128)(2,1)} async-done(((bf16[64,1792]{1,0:T(8,128)(2,1)}), bf16[64,14336]{1,0:T(8,128)(2,1)}) %all-gather.8.cloned.1.call-update) | async-done | bytes 1835024 | tf_op jit(solution)/shard_map/all_gather | solution.py:21
  283.7 8.3 fusion.165
  292.1 31.4 %all_gather.33 = bf16[64,4096]{1,0:T(8,128)(2,1)S(1)} all-gather(bf16[64,512]{1,0:T(8,128)(2,1)S(1)} %reduce_sum.221), channel_id=1, replica_groups=mesh['section'=4,'tensor'=8] {'tensor'}, dimensions={1}, use_global_device_ids=true | all-gather | bytes 589824 | tf_op jit(solution)/shard_map/all_gather | solution.py:33
  323.9 7.8 fusion.26
  331.7 14.3 %fusion.73 = bf16[64,4096]{1,0:T(8,128)(2,1)} fusion(bf16[1,1792,4096]{2,1,0:T(8,128)(2,1)} %param.11, bf16[1,2,1792,4096]{3,2,1,0:T(8,128)(2,1)} %param.10, f32[64,1792]{1,0:T(8,128)S(1)} %fusion.26, bf16[64,4096]{1,0:T(8,128)(2,1)S(1)} %get-tuple-element.25, f32[64]{0:T(128)S(1)} %add_rsqrt_fusion.6, f32[4096]{0:T(1024)S(1)} %bitcast.193), kind=kOutput, calls=%fused_computation.71 | convolution fusion | flops 1881047040 | bytes 30884096 | tf_op jit(solution)/shard_map/dot_general | solution.py:16
  346.8 70.6 %all-reduce.8.cloned.1.call-done = bf16[64,4096]{1,0:T(8,128)(2,1)} async-done(((bf16[64,4096]{1,0:T(8,128)(2,1)}), bf16[64,4096]{1,0:T(8,128)(2,1)}) %all-reduce.8.cloned.1.call-update) | async-done | bytes 524304 | tf_op jit(solution)/shard_map/psum | solution.py:17
  418.7 1.5 collective-permute-start.1
  420.2 1.3 collective-permute-done.1
  421.8 7.8 fusion.44
  429.6 8.6 fusion.136
  439.0 53.1 %all-gather.10.cloned.1.call-done = bf16[64,14336]{1,0:T(8,128)(2,1)} async-done(((bf16[64,1792]{1,0:T(8,128)(2,1)}), bf16[64,14336]{1,0:T(8,128)(2,1)}) %all-gather.10.cloned.1.call-update) | async-done | bytes 1835024 | tf_op jit(solution)/shard_map/all_gather | solution.py:21
  492.2 8.3 fusion.168
  500.5 31.4 %all_gather.35 = bf16[64,4096]{1,0:T(8,128)(2,1)S(1)} all-gather(bf16[64,512]{1,0:T(8,128)(2,1)S(1)} %reduce_sum.225), channel_id=1, replica_groups=mesh['section'=4,'tensor'=8] {'tensor'}, dimensions={1}, use_global_device_ids=true | all-gather | bytes 589824 | tf_op jit(solution)/shard_map/all_gather | solution.py:33
  532.4 7.8 fusion.24
  540.2 14.3 %fusion.76 = bf16[64,4096]{1,0:T(8,128)(2,1)} fusion(bf16[1,1792,4096]{2,1,0:T(8,128)(2,1)} %param.11, bf16[1,2,1792,4096]{3,2,1,0:T(8,128)(2,1)} %param.10, f32[64,1792]{1,0:T(8,128)S(1)} %fusion.24, bf16[64,4096]{1,0:T(8,128)(2,1)S(1)} %get-tuple-element.21, f32[64]{0:T(128)S(1)} %add_rsqrt_fusion.4, f32[4096]{0:T(1024)S(1)} %bitcast.195), kind=kOutput, calls=%fused_computation.72 | convolution fusion | flops 1881047040 | bytes 30884096 | tf_op jit(solution)/shard_map/dot_general | solution.py:16
  555.3 70.5 %all-reduce.10.cloned.1.call-done = bf16[64,4096]{1,0:T(8,128)(2,1)} async-done(((bf16[64,4096]{1,0:T(8,128)(2,1)}), bf16[64,4096]{1,0:T(8,128)(2,1)}) %all-reduce.10.cloned.1.call-update) | async-done | bytes 524304 | tf_op jit(solution)/shard_map/psum | solution.py:17
  627.1 1.7 collective-permute-start.2
  630.2 7.8 fusion.42
  638.1 8.6 fusion.133
  647.4 53.3 %all-gather.12.cloned.1.call-done = bf16[64,14336]{1,0:T(8,128)(2,1)} async-done(((bf16[64,1792]{1,0:T(8,128)(2,1)}), bf16[64,14336]{1,0:T(8,128)(2,1)}) %all-gather.12.cloned.1.call-update) | async-done | bytes 1835024 | tf_op jit(solution)/shard_map/all_gather | solution.py:21
  700.6 8.3 fusion.171
  709.0 31.4 %all_gather.37 = bf16[64,4096]{1,0:T(8,128)(2,1)S(1)} all-gather(bf16[64,512]{1,0:T(8,128)(2,1)S(1)} %reduce_sum.229), channel_id=1, replica_groups=mesh['section'=4,'tensor'=8] {'tensor'}, dimensions={1}, use_global_device_ids=true | all-gather | bytes 589824 | tf_op jit(solution)/shard_map/all_gather | solution.py:33
  740.8 7.8 fusion.22
  748.7 14.3 %fusion.79 = bf16[64,4096]{1,0:T(8,128)(2,1)} fusion(bf16[1,1792,4096]{2,1,0:T(8,128)(2,1)} %param.11, bf16[1,2,1792,4096]{3,2,1,0:T(8,128)(2,1)} %param.10, f32[64,1792]{1,0:T(8,128)S(1)} %fusion.22, bf16[64,4096]{1,0:T(8,128)(2,1)S(1)} %get-tuple-element.17, f32[64]{0:T(128)S(1)} %add_rsqrt_fusion.2, f32[4096]{0:T(1024)S(1)} %bitcast.197), kind=kOutput, calls=%fused_computation.73 | convolution fusion | flops 1881047040 | bytes 30884096 | tf_op jit(solution)/shard_map/dot_general | solution.py:16
  763.7 70.7 %all-reduce.12.cloned.1.call-done = bf16[64,4096]{1,0:T(8,128)(2,1)} async-done(((bf16[64,4096]{1,0:T(8,128)(2,1)}), bf16[64,4096]{1,0:T(8,128)(2,1)}) %all-reduce.12.cloned.1.call-update) | async-done | bytes 524304 | tf_op jit(solution)/shard_map/psum | solution.py:17
  835.6 1.5 collective-permute-start.3
  837.1 1.3 collective-permute-done.3
  838.7 7.8 fusion.40
  846.6 8.6 fusion.130
  856.9 52.2 %all-gather.14.cloned.1.call-done = bf16[64,14336]{1,0:T(8,128)(2,1)} async-done(((bf16[64,1792]{1,0:T(8,128)(2,1)}), bf16[64,14336]{1,0:T(8,128)(2,1)}) %all-gather.14.cloned.1.call-update) | async-done | bytes 1835024 | tf_op jit(solution)/shard_map/all_gather | solution.py:21
  909.2 8.3 fusion.174
  917.5 31.4 %all_gather.39 = bf16[64,4096]{1,0:T(8,128)(2,1)S(1)} all-gather(bf16[64,512]{1,0:T(8,128)(2,1)S(1)} %reduce_sum.233), channel_id=1, replica_groups=mesh['section'=4,'tensor'=8] {'tensor'}, dimensions={1}, use_global_device_ids=true | all-gather | bytes 589824 | tf_op jit(solution)/shard_map/all_gather | solution.py:33
  949.3 7.8 fusion.20
  957.2 14.3 %fusion.82 = bf16[64,4096]{1,0:T(8,128)(2,1)} fusion(bf16[1,1792,4096]{2,1,0:T(8,128)(2,1)} %param.11, bf16[1,2,1792,4096]{3,2,1,0:T(8,128)(2,1)} %param.10, f32[64,1792]{1,0:T(8,128)S(1)} %fusion.20, f32[64,4096]{1,0:T(8,128)S(1)} %get-tuple-element.13, f32[64]{0:T(128)S(1)} %add_rsqrt_fusion, f32[4096]{0:T(1024)S(1)} %bitcast.199), kind=kOutput, calls=%fused_computation.74 | convolution fusion | flops 1880784896 | bytes 31408384 | tf_op jit(solution)/shard_map/dot_general | solution.py:16
  973.2 69.6 %all-reduce.14.cloned.1.call-done = bf16[64,4096]{1,0:T(8,128)(2,1)} async-done(((bf16[64,4096]{1,0:T(8,128)(2,1)}), bf16[64,4096]{1,0:T(8,128)(2,1)}) %all-reduce.14.cloned.1.call-update) | async-done | bytes 524304 | tf_op jit(solution)/shard_map/psum | solution.py:17
  (82 shorter events, 22.5 us)
Async XLA Ops:
  6.5 10.2 copy-start
  6.5 68.7 %all-gather.6.cloned.1.call-start = ((), (), s32[]{:S(2)}) async-start(), calls=%async_computation | async-start | bytes 2064384 | tf_op jit(solution)/shard_map/all_gather | solution.py:21
  16.8 8.8 copy-start.3
  16.8 10.2 copy-start.4
  25.5 183.5 %all-reduce.6.cloned.1.call-start = ((), (), s32[]{:S(2)}) async-start(), calls=%async_computation.1 | async-start | bytes 1048576 | tf_op jit(solution)/shard_map/psum | solution.py:17
  137.6 146.1 %all-gather.8.cloned.1.call-start = ((), (), s32[]{:S(2)}) async-start(), calls=%async_computation.2 | async-start | bytes 2064384 | tf_op jit(solution)/shard_map/all_gather | solution.py:21
  210.2 2.8 collective-permute-start
  229.8 187.6 %all-reduce.8.cloned.1.call-start = ((), (), s32[]{:S(2)}) async-start(), calls=%async_computation.3 | async-start | bytes 1048576 | tf_op jit(solution)/shard_map/psum | solution.py:17
  346.1 146.1 %all-gather.10.cloned.1.call-start = ((), (), s32[]{:S(2)}) async-start(), calls=%async_computation.4 | async-start | bytes 2064384 | tf_op jit(solution)/shard_map/all_gather | solution.py:21
  418.7 2.8 collective-permute-start.1
  438.3 187.6 %all-reduce.10.cloned.1.call-start = ((), (), s32[]{:S(2)}) async-start(), calls=%async_computation.5 | async-start | bytes 1048576 | tf_op jit(solution)/shard_map/psum | solution.py:17
  554.6 146.1 %all-gather.12.cloned.1.call-start = ((), (), s32[]{:S(2)}) async-start(), calls=%async_computation.6 | async-start | bytes 2064384 | tf_op jit(solution)/shard_map/all_gather | solution.py:21
  627.1 1.7 copy-start.1
  627.1 2.8 collective-permute-start.2
  646.8 187.6 %all-reduce.12.cloned.1.call-start = ((), (), s32[]{:S(2)}) async-start(), calls=%async_computation.7 | async-start | bytes 1048576 | tf_op jit(solution)/shard_map/psum | solution.py:17
  763.0 146.1 %all-gather.14.cloned.1.call-start = ((), (), s32[]{:S(2)}) async-start(), calls=%async_computation.8 | async-start | bytes 2064384 | tf_op jit(solution)/shard_map/all_gather | solution.py:21
  835.6 3.1 copy-start.2
  835.6 2.8 collective-permute-start.3
  855.3 187.6 %all-reduce.14.cloned.1.call-start = ((), (), s32[]{:S(2)}) async-start(), calls=%async_computation.9 | async-start | bytes 1048576 | tf_op jit(solution)/shard_map/psum | solution.py:17
Sparse Core Ops, SparseCore 0:
  25.6 49.5 all-gather.5
  137.7 71.1 all-reduce.5
  230.0 53.7 all-gather.7
  346.2 71.1 all-reduce.7
  438.4 53.7 all-gather.9
  554.7 71.1 all-reduce.9
  646.9 53.7 all-gather.11
  763.1 71.1 all-reduce.11
  855.4 53.7 all-gather.13
  971.6 71.1 all-reduce.13
where the time goes:
time: 1060 us; the launch traced here: 1050 us
  waiting for transfers between devices  615 us (58%)
  matrix products  235 us (22%)
  blocking collectives  157 us (15%)
  other arithmetic  20.4 us (2%)
  between operations  15.6 us (1%)
    psum x5, waiting for transfers between devices, finish_sum(): lax.psum(partial_value.astype(jnp.bfloat16), 'tensor').astype(jnp.float32)  351 us
    all_gather x5, waiting for transfers between devices, finish_columns(): full_hidden = lax.all_gather(hidden, 'tensor', axis=1, tiled=True)  259 us
    all_gather x5, blocking collectives, finish_columns(): lax.all_gather(column_sum.astype(jnp.bfloat16), 'tensor', axis=1, tiled=T...  157 us
    dot_general x10, matrix products, apply_layer(): lax.dot_general(normed, w_pair[0], (((1,), (1,)), ((), ())), preferred_el...  78.6 us
    dot_general x5, matrix products, finish_sum(): partial_value = jnp.dot(hidden, w_down, preferred_element_type=jnp.float32)  71.7 us
    dot_general x5, matrix products, apply_layer(): lax.dot_general(normed, w_pair[1], (((1,), (1,)), ((), ())), preferred_el...  43.2 us
    dot_general x5, matrix products, finish_columns(): jnp.einsum('rbf,bfd->brd', full_hidden.reshape(row_count, blocks, block_w...  41.4 us
  transfers between devices with their start and end apart: 14, of which 14 were waited for; matrix products, arithmetic and copies ran while one was open for 1% of the time, Pallas kernels for 0%

commit v1 on v0

--- a/solution.py
+++ b/solution.py
@@ -4,6 +4,17 @@
 from jax.sharding import PartitionSpec as P
 
 NORM_EPS = 0.25
+
+
+def around_the_ring(array, axis, along):
+    size = lax.axis_size(axis)
+    route = [(i, (i + 1) % size) for i in range(size)]
+    parts = [array]
+    for far in range(1, size):
+        parts = [lax.ppermute(parts[0], axis, route), *parts]
+    whole = jnp.concatenate(parts, axis=along)
+    offset = (lax.axis_index(axis) + 1) * parts[-1].shape[along]
+    return jnp.roll(whole, offset, axis=along)
 
 
 def passed_along(block, axis, distance):
@@ -18,7 +29,7 @@
 
 
 def finish_columns(hidden, w_down):
-    full_hidden = lax.all_gather(hidden, "tensor", axis=1, tiled=True)
+    full_hidden = around_the_ring(hidden, "tensor", 1)
     row_count = full_hidden.shape[0]
     blocks = lax.axis_size("tensor")
     block_width = full_hidden.shape[1] // blocks

time: 1060 us -> 1150 us (1.085)
  waiting for transfers between devices: 615 us -> 699 us
    ppermute x0 -> x35, waiting for transfers between devices: none -> 319 us  [around_the_ring(): parts = [lax.ppermute(parts[0], axis, route), *parts]]
    all_gather x5 -> x0, waiting for transfers between devices: 259 us -> none  [finish_columns(): full_hidden = lax.all_gather(hidden, 'tensor', axis=1, tiled=True)]
    psum x5, waiting for transfers between devices: 351 us -> 374 us  [finish_sum(): lax.psum(partial_value.astype(jnp.bfloat16), 'tensor').astype(jnp.float32)]
  transfers between devices with their start and end apart: 14 -> 44, of which waited for: 14 -> 44; matrix products, arithmetic and copies ran while one was open for 1% -> 1% of each run, Pallas kernels for 0% -> 0%
where the time goes in v1:
time: 1150 us; the launch traced here: 1140 us
  waiting for transfers between devices  699 us (61%)
  matrix products  229 us (20%)
  blocking collectives  157 us (14%)
  other arithmetic  27.1 us (2%)
  between operations  15.8 us (1%)
  starting transfers between devices  12.8 us (1%)
    psum x5, waiting for transfers between devices, finish_sum(): lax.psum(partial_value.astype(jnp.bfloat16), 'tensor').astype(jnp.float32)  374 us
    ppermute x35, waiting for transfers between devices, around_the_ring(): parts = [lax.ppermute(parts[0], axis, route), *parts]  319 us
    all_gather x5, blocking collectives, finish_columns(): lax.all_gather(column_sum.astype(jnp.bfloat16), 'tensor', axis=1, tiled=T...  157 us
    dot_general x10, matrix products, apply_layer(): lax.dot_general(normed, w_pair[0], (((1,), (1,)), ((), ())), preferred_el...  78.6 us
    dot_general x5, matrix products, finish_sum(): partial_value = jnp.dot(hidden, w_down, preferred_element_type=jnp.float32)  71.7 us
    dot_general x5, matrix products, apply_layer(): lax.dot_general(normed, w_pair[1], (((1,), (1,)), ((), ())), preferred_el...  39.8 us
    dot_general x5, matrix products, finish_columns(): jnp.einsum('rbf,bfd->brd', full_hidden.reshape(row_count, blocks, block_w...  38.8 us
  transfers between devices with their start and end apart: 44, of which 44 were waited for; matrix products, arithmetic and copies ran while one was open for 1% of the time, Pallas kernels for 0%

profile of v1, /device:TPU:0, one launch (start us, length us, event | category | flops | bytes accessed | tf_op | source)
XLA Modules:
  0.0 1142.6 jit_solution(9261591487575793518)
XLA Ops:
  8.7 8.0 fusion.48
  27.8 8.6 collective-permute-done
  36.4 9.5 collective-permute-done.1
  45.9 8.7 collective-permute-done.2
  54.6 8.7 collective-permute-done.3
  63.3 8.7 collective-permute-done.4
  72.0 9.6 collective-permute-done.5
  99.8 31.5 %all_gather.15 = bf16[64,4096]{1,0:T(8,128)(2,1)S(1)} all-gather(bf16[64,512]{1,0:T(8,128)(2,1)S(1)} %reduce_sum.216), channel_id=1, replica_groups=mesh['section'=4,'tensor'=8] {'tensor'}, dimensions={1}, use_global_device_ids=true | all-gather | bytes 589824 | tf_op jit(solution)/shard_map/all_gather | solution.py:44
  139.6 14.3 %fusion.70 = bf16[64,4096]{1,0:T(8,128)(2,1)} fusion(bf16[1,1792,4096]{2,1,0:T(8,128)(2,1)} %param.13, bf16[1,2,1792,4096]{3,2,1,0:T(8,128)(2,1)} %param.12, f32[64,1792]{1,0:T(8,128)S(1)} %fusion.28, bf16[64,4096]{1,0:T(8,128)(2,1)S(1)} %get-tuple-element.30, f32[4096]{0:T(1024)S(1)} %bitcast.191, f32[64]{0:T(128)S(1)} %add_rsqrt_fusion.8), kind=kOutput, calls=%fused_computation.70 | convolution fusion | flops 1881047040 | bytes 30884096 | tf_op jit(solution)/shard_map/dot_general | solution.py:27
  155.3 68.8 %all-reduce.6.cloned.1.call-done = bf16[64,4096]{1,0:T(8,128)(2,1)} async-done(((bf16[64,4096]{1,0:T(8,128)(2,1)}), bf16[64,4096]{1,0:T(8,128)(2,1)}) %all-reduce.6.cloned.1.call-update) | async-done | bytes 524304 | tf_op jit(solution)/shard_map/psum | solution.py:28
  245.0 8.0 collective-permute-done.8
  253.0 8.7 collective-permute-done.9
  261.7 8.7 collective-permute-done.10
  270.5 8.8 collective-permute-done.11
  279.3 9.9 collective-permute-done.12
  289.2 11.1 collective-permute-done.13
  301.1 9.7 collective-permute-done.14
  320.3 31.2 %all_gather.16 = bf16[64,4096]{1,0:T(8,128)(2,1)S(1)} all-gather(bf16[64,512]{1,0:T(8,128)(2,1)S(1)} %reduce_sum.221), channel_id=1, replica_groups=mesh['section'=4,'tensor'=8] {'tensor'}, dimensions={1}, use_global_device_ids=true | all-gather | bytes 589824 | tf_op jit(solution)/shard_map/all_gather | solution.py:44
  359.7 14.3 %fusion.73 = bf16[64,4096]{1,0:T(8,128)(2,1)} fusion(bf16[1,1792,4096]{2,1,0:T(8,128)(2,1)} %param.13, bf16[1,2,1792,4096]{3,2,1,0:T(8,128)(2,1)} %param.12, f32[64,1792]{1,0:T(8,128)S(1)} %fusion.26, bf16[64,4096]{1,0:T(8,128)(2,1)S(1)} %get-tuple-element.26, f32[64]{0:T(128)S(1)} %add_rsqrt_fusion.6, f32[4096]{0:T(1024)S(1)} %bitcast.193), kind=kOutput, calls=%fused_computation.71 | convolution fusion | flops 1881047040 | bytes 30884096 | tf_op jit(solution)/shard_map/dot_general | solution.py:27
  374.7 76.5 %all-reduce.8.cloned.1.call-done = bf16[64,4096]{1,0:T(8,128)(2,1)} async-done(((bf16[64,4096]{1,0:T(8,128)(2,1)}), bf16[64,4096]{1,0:T(8,128)(2,1)}) %all-reduce.8.cloned.1.call-update) | async-done | bytes 524304 | tf_op jit(solution)/shard_map/psum | solution.py:28
  472.2 8.0 collective-permute-done.16
  480.2 8.7 collective-permute-done.17
  488.9 8.7 collective-permute-done.18
  497.6 8.8 collective-permute-done.19
  506.4 9.9 collective-permute-done.20
  516.4 11.1 collective-permute-done.21
  528.2 9.6 collective-permute-done.22
  547.2 31.4 %all_gather.17 = bf16[64,4096]{1,0:T(8,128)(2,1)S(1)} all-gather(bf16[64,512]{1,0:T(8,128)(2,1)S(1)} %reduce_sum.225), channel_id=1, replica_groups=mesh['section'=4,'tensor'=8] {'tensor'}, dimensions={1}, use_global_device_ids=true | all-gather | bytes 589824 | tf_op jit(solution)/shard_map/all_gather | solution.py:44
  586.8 14.3 %fusion.76 = bf16[64,4096]{1,0:T(8,128)(2,1)} fusion(bf16[1,1792,4096]{2,1,0:T(8,128)(2,1)} %param.13, bf16[1,2,1792,4096]{3,2,1,0:T(8,128)(2,1)} %param.12, f32[64,1792]{1,0:T(8,128)S(1)} %fusion.24, bf16[64,4096]{1,0:T(8,128)(2,1)S(1)} %get-tuple-element.22, f32[64]{0:T(128)S(1)} %add_rsqrt_fusion.4, f32[4096]{0:T(1024)S(1)} %bitcast.195), kind=kOutput, calls=%fused_computation.72 | convolution fusion | flops 1881047040 | bytes 30884096 | tf_op jit(solution)/shard_map/dot_general | solution.py:27
  601.9 76.4 %all-reduce.10.cloned.1.call-done = bf16[64,4096]{1,0:T(8,128)(2,1)} async-done(((bf16[64,4096]{1,0:T(8,128)(2,1)}), bf16[64,4096]{1,0:T(8,128)(2,1)}) %all-reduce.10.cloned.1.call-update) | async-done | bytes 524304 | tf_op jit(solution)/shard_map/psum | solution.py:28
  699.3 8.0 collective-permute-done.24
  707.3 8.7 collective-permute-done.25
  716.0 8.7 collective-permute-done.26
  724.7 8.8 collective-permute-done.27
  733.5 9.9 collective-permute-done.28
  743.5 11.1 collective-permute-done.29
  755.4 9.7 collective-permute-done.30
  774.5 31.2 %all_gather.18 = bf16[64,4096]{1,0:T(8,128)(2,1)S(1)} all-gather(bf16[64,512]{1,0:T(8,128)(2,1)S(1)} %reduce_sum.229), channel_id=1, replica_groups=mesh['section'=4,'tensor'=8] {'tensor'}, dimensions={1}, use_global_device_ids=true | all-gather | bytes 589824 | tf_op jit(solution)/shard_map/all_gather | solution.py:44
  813.9 14.4 %fusion.79 = bf16[64,4096]{1,0:T(8,128)(2,1)} fusion(bf16[1,1792,4096]{2,1,0:T(8,128)(2,1)} %param.13, bf16[1,2,1792,4096]{3,2,1,0:T(8,128)(2,1)} %param.12, f32[64,1792]{1,0:T(8,128)S(1)} %fusion.22, bf16[64,4096]{1,0:T(8,128)(2,1)S(1)} %get-tuple-element.18, f32[64]{0:T(128)S(1)} %add_rsqrt_fusion.2, f32[4096]{0:T(1024)S(1)} %bitcast.197), kind=kOutput, calls=%fused_computation.73 | convolution fusion | flops 1881047040 | bytes 30884096 | tf_op jit(solution)/shard_map/dot_general | solution.py:27
  829.0 76.5 %all-reduce.12.cloned.1.call-done = bf16[64,4096]{1,0:T(8,128)(2,1)} async-done(((bf16[64,4096]{1,0:T(8,128)(2,1)}), bf16[64,4096]{1,0:T(8,128)(2,1)}) %all-reduce.12.cloned.1.call-update) | async-done | bytes 524304 | tf_op jit(solution)/shard_map/psum | solution.py:28
  934.5 8.7 collective-permute-done.33
  943.2 8.7 collective-permute-done.34
  960.8 9.9 collective-permute-done.36
  970.8 11.3 collective-permute-done.37
  982.1 10.3 collective-permute-done.38
  1002.7 31.5 %all_gather.19 = bf16[64,4096]{1,0:T(8,128)(2,1)S(1)} all-gather(bf16[64,512]{1,0:T(8,128)(2,1)S(1)} %reduce_sum.233), channel_id=1, replica_groups=mesh['section'=4,'tensor'=8] {'tensor'}, dimensions={1}, use_global_device_ids=true | all-gather | bytes 589824 | tf_op jit(solution)/shard_map/all_gather | solution.py:44
  1042.5 14.4 %fusion.82 = bf16[64,4096]{1,0:T(8,128)(2,1)} fusion(bf16[1,1792,4096]{2,1,0:T(8,128)(2,1)} %param.13, bf16[1,2,1792,4096]{3,2,1,0:T(8,128)(2,1)} %param.12, f32[64,1792]{1,0:T(8,128)S(1)} %fusion.20, f32[64,4096]{1,0:T(8,128)S(1)} %get-tuple-element.14, f32[64]{0:T(128)S(1)} %add_rsqrt_fusion, f32[4096]{0:T(1024)S(1)} %bitcast.199), kind=kOutput, calls=%fused_computation.74 | convolution fusion | flops 1880784896 | bytes 31408384 | tf_op jit(solution)/shard_map/dot_general | solution.py:27
  1057.7 76.2 %all-reduce.14.cloned.1.call-done = bf16[64,4096]{1,0:T(8,128)(2,1)} async-done(((bf16[64,4096]{1,0:T(8,128)(2,1)}), bf16[64,4096]{1,0:T(8,128)(2,1)}) %all-reduce.14.cloned.1.call-update) | async-done | bytes 524304 | tf_op jit(solution)/shard_map/psum | solution.py:28
  (180 shorter events, 218.4 us)
Async XLA Ops:
  6.5 217.5 %all-reduce.6.cloned.1.call-start = ((), (), s32[]{:S(2)}) async-start(), calls=%async_computation | async-start | bytes 1048576 | tf_op jit(solution)/shard_map/psum | solution.py:28
  8.7 8.0 copy-start
  16.7 64.9 %copy-start.2 = (s32[4]{0:T(128)S(1)}, s32[4]{0:T(128)}, u32[]{:S(2)}) copy-start(s32[4]{0:T(128)} %param.16) | copy-start | bytes 52
  16.7 66.3 %copy-start.3 = (s32[2]{0:T(128)S(1)}, s32[2]{0:T(128)}, u32[]{:S(2)}) copy-start(s32[2]{0:T(128)} %param.17) | copy-start | bytes 28
  24.7 11.7 %collective-permute-start = (bf16[64,1792]{1,0:T(8,128)(2,1)S(1)}, bf16[64,1792]{1,0:T(8,128)(2,1)S(1)}, u32[]{:S(2)}, u32[]{:S(2)}) collective-permute-start(bf16[64,1792]{1,0:T(8,128)(2,1)S(1)} %fusion.142), channel_id=1, source_target_pairs={{0,1},{1,2},{2,3},{3,4},{4,5},{5,6},{6,7},{7,0},{8,9},{9,10},{10,1... | collective-permute-start | bytes 688136 | tf_op jit(solution)/shard_map/ppermute | solution.py:14
  36.4 9.5 collective-permute-start.1
  45.9 8.7 collective-permute-start.2
  54.6 8.7 collective-permute-start.3
  63.3 8.7 collective-permute-start.4
  72.0 9.6 collective-permute-start.5
  81.7 8.7 collective-permute-start.6
  153.9 297.3 %all-reduce.8.cloned.1.call-start = ((), (), s32[]{:S(2)}) async-start(), calls=%async_computation.1 | async-start | bytes 1048576 | tf_op jit(solution)/shard_map/psum | solution.py:28
  225.3 2.8 collective-permute-start.7
  244.2 8.8 collective-permute-start.8
  253.0 8.7 collective-permute-start.9
  261.7 8.7 collective-permute-start.10
  270.5 8.8 collective-permute-start.11
  279.3 10.0 collective-permute-start.12
  289.2 11.1 collective-permute-start.13
  300.3 10.6 collective-permute-start.14
  374.1 304.2 %all-reduce.10.cloned.1.call-start = ((), (), s32[]{:S(2)}) async-start(), calls=%async_computation.2 | async-start | bytes 1048576 | tf_op jit(solution)/shard_map/psum | solution.py:28
  452.5 2.8 collective-permute-start.15
  471.4 8.8 collective-permute-start.16
  480.2 8.7 collective-permute-start.17
  488.9 8.7 collective-permute-start.18
  497.6 8.8 collective-permute-start.19
  506.4 9.9 collective-permute-start.20
  516.4 11.1 collective-permute-start.21
  527.4 10.3 collective-permute-start.22
  601.2 304.3 %all-reduce.12.cloned.1.call-start = ((), (), s32[]{:S(2)}) async-start(), calls=%async_computation.3 | async-start | bytes 1048576 | tf_op jit(solution)/shard_map/psum | solution.py:28
  679.6 1.3 copy-start.1
  679.6 2.8 collective-permute-start.23
  698.5 8.8 collective-permute-start.24
  707.3 8.7 collective-permute-start.25
  716.0 8.7 collective-permute-start.26
  724.7 8.8 collective-permute-start.27
  733.5 9.9 collective-permute-start.28
  743.5 11.1 collective-permute-start.29
  754.6 10.5 collective-permute-start.30
  828.3 305.6 %all-reduce.14.cloned.1.call-start = ((), (), s32[]{:S(2)}) async-start(), calls=%async_computation.4 | async-start | bytes 1048576 | tf_op jit(solution)/shard_map/psum | solution.py:28
  906.8 2.8 collective-permute-start.31
  925.7 8.8 collective-permute-start.32
  934.5 8.7 collective-permute-start.33
  943.2 8.7 collective-permute-start.34
  951.9 8.8 collective-permute-start.35
  960.7 10.1 collective-permute-start.36
  970.8 11.3 collective-permute-start.37
  982.1 10.3 collective-permute-start.38
Sparse Core Ops, SparseCore 0:
  154.0 69.9 all-reduce.5
  374.2 76.9 all-reduce.7
  601.3 76.9 all-reduce.9
  828.4 77.0 all-reduce.11
  1057.0 76.8 all-reduce.13
